TPU v7x, 32 devices: a whole 2x2x4 slice. The times are simulated.
32 devices in a mesh: chain: 16 (over z, y, x), grp: 2 (over core).
Axes of the slice: x: 2, y: 2, z: 4, core: 2. Of those that a mesh axis runs over, the one named last changes fastest.
Arguments:
- codes: bfloat16 [2, 16384, 6144], P(None, ('chain', 'grp')), may hold values from -6 to 6
- exponents: int32 [2, 512, 6144], P(None, ('chain', 'grp')), may hold values from -2 to 2
- column_map: int32 [32], replicated, may hold values from 0 to 31, each once
- row_order: int32 [32], replicated, may hold values from 0 to 31, each once
Outputs:
- rollout: bfloat16 [2, 6144, 16384], P(None, ('chain', 'grp'))
- block_sums: float32 [2, 6144, 512], P(None, ('chain', 'grp'))
All inputs are finite; a program needn't handle non-finite values.
Results may differ from a plain program's by a relative error of at most 0.001.
Values may be sent and summed in bfloat16 or wider, within the bound.
A program may use at most 128 MiB of HBM per device.

v0:
```python
import functools

import jax
import jax.numpy as jnp
from jax import lax
from jax.experimental import pallas as pl
from jax.experimental.pallas import tpu as pltpu
from jax.sharding import PartitionSpec as P

MESH = pl.DeviceIdType.MESH
BLOCK = 32
LANES = 128


def partner(me, step, devices):
    if devices & (devices - 1):
        return lax.rem(me + step, devices)
    peer, bit = 0, 1
    while bit < devices:
        peer = peer + lax.rem(me // bit + step // bit, 2) * bit
        bit *= 2
    return peer


def origin(me, step, devices):
    if devices & (devices - 1):
        return lax.rem(me - step + devices, devices)
    return partner(me, step, devices)


def turn_of(index, devices):
    if devices % 2:
        return index + 1
    odd = lax.rem(index, 2)
    return (index + odd) // 2 + (1 - odd) * (devices // 2)


class Traffic:
    def __init__(self, devices, grp_size, source, arrived, send_sems, recv_sems):
        self.devices, self.grp_size = devices, grp_size
        self.source, self.arrived = source, arrived
        self.send_sems, self.recv_sems = send_sems, recv_sems
        self.me = lax.axis_index("chain") * grp_size + lax.axis_index("grp")

    def copy(self, step, other, slot):
        return pltpu.make_async_remote_copy(
            src_ref=self.source(step, other),
            dst_ref=self.arrived.at[slot],
            send_sem=self.send_sems.at[step],
            recv_sem=self.recv_sems.at[step],
            device_id=(other // self.grp_size, lax.rem(other, self.grp_size)),
            device_id_type=MESH,
        )

    def send(self, step):
        return self.copy(step, partner(self.me, step, self.devices), self.me)

    def finish(self):
        @pl.loop(1, self.devices)
        def _(step):
            sender = origin(self.me, step, self.devices)
            self.copy(step, sender, sender).wait_recv()

        @pl.loop(1, self.devices)
        def _(step):
            self.send(step).wait_send()


def fused_kernel(
    devices, grp_size, column_map, codes, exponents, arrived,
    codes_in, exponents_in, turned, sending, load_sems, send_sems, recv_sems, own_sem,
):
    pairs, layers, rows, pair = codes_in.shape
    col_width = pair // 2

    def loads(index):
        columns = pl.ds(pl.multiple_of(index * pair, LANES), pair)
        return (
            pltpu.make_async_copy(codes.at[:, :, columns], codes_in.at[index], load_sems.at[0, index]),
            pltpu.make_async_copy(exponents.at[:, :, columns], exponents_in.at[index], load_sems.at[1, index]),
        )

    @pl.loop(0, pairs)
    def _(index):
        for load in loads(index):
            load.start()

    @pl.loop(0, pairs)
    def _(index):
        for load in loads(index):
            load.wait()

    traffic = Traffic(
        devices, grp_size, lambda step, other: sending.at[step], arrived, send_sems, recv_sems
    )

    def fill(step):
        column = column_map[partner(traffic.me, step, devices)]
        which = column // 2
        for layer in range(layers):
            scaling = jnp.exp2(exponents_in[which, layer].astype(jnp.float32)).astype(jnp.bfloat16)
            for first in range(0, rows, LANES):
                pieces = []
                for row in range(first, first + LANES, BLOCK):
                    block = row // BLOCK
                    values = codes_in[which, layer, row : row + BLOCK, :]
                    pieces.append(values * scaling[block : block + 1, :])
                both = jnp.concatenate(pieces, axis=0).T
                turned[0, layer, :, first : first + LANES] = both[:col_width]
                turned[1, layer, :, first : first + LANES] = both[col_width:]
        sending[step] = turned[lax.rem(column, 2)]

    fill(turn_of(0, devices))

    @pl.loop(1, devices - 1)
    def _(index):
        fill(turn_of(index, devices))
        traffic.send(turn_of(index - 1, devices)).start()

    fill(0)
    traffic.send(turn_of(devices - 2, devices)).start()
    own = pltpu.make_async_copy(sending.at[0], arrived.at[traffic.me], own_sem)
    own.start()
    own.wait()
    traffic.finish()


def exchange_kernel(devices, grp_size, outgoing, arrived, own, send_sems, recv_sems, own_sems):
    traffic = Traffic(
        devices, grp_size, lambda step, other: outgoing.at[other], arrived, send_sems, recv_sems
    )

    @pl.loop(0, devices - 1)
    def _(index):
        traffic.send(turn_of(index, devices)).start()

    take = pltpu.make_async_copy(outgoing.at[traffic.me], own, own_sems.at[0])
    take.start()
    take.wait()
    put = pltpu.make_async_copy(own, arrived.at[traffic.me], own_sems.at[1])
    put.start()
    put.wait()
    traffic.finish()


def exchange(codes, exponents, column_map, devices, grp_size):
    layers, rows, width = codes.shape
    col_width = width // devices
    block = (layers, col_width, rows)
    shape = jax.ShapeDtypeStruct((devices, *block), jnp.bfloat16)
    anywhere = pl.BlockSpec(memory_space=pl.ANY)
    peers = pltpu.SemaphoreType.DMA((devices,))
    if col_width % 64 or rows % LANES or devices % 2:
        scaling = jnp.exp2(exponents.astype(jnp.float32))
        values = (codes.astype(jnp.float32) * jnp.repeat(scaling, BLOCK, axis=1)).astype(jnp.bfloat16)
        values = values.reshape(layers, rows, devices, col_width)
        outgoing = jnp.take(values.transpose(2, 0, 3, 1), column_map, axis=0)
        return pl.pallas_call(
            functools.partial(exchange_kernel, devices, grp_size),
            out_shape=shape,
            in_specs=[anywhere],
            out_specs=anywhere,
            scratch_shapes=[pltpu.VMEM(block, jnp.bfloat16), peers, peers, pltpu.SemaphoreType.DMA((2,))],
            compiler_params=pltpu.CompilerParams(has_side_effects=True),
        )(outgoing)
    pairs = devices // 2
    return pl.pallas_call(
        functools.partial(fused_kernel, devices, grp_size),
        out_shape=shape,
        in_specs=[pl.BlockSpec(memory_space=pltpu.SMEM), anywhere, anywhere],
        out_specs=anywhere,
        scratch_shapes=[
            pltpu.VMEM((pairs, layers, rows, 2 * col_width), codes.dtype),
            pltpu.VMEM((pairs, layers, rows // BLOCK, 2 * col_width), exponents.dtype),
            pltpu.VMEM((2, *block), jnp.bfloat16),
            pltpu.VMEM((devices, *block), jnp.bfloat16),
            pltpu.SemaphoreType.DMA((2, pairs)),
            peers,
            peers,
            pltpu.SemaphoreType.DMA,
        ],
        compiler_params=pltpu.CompilerParams(has_side_effects=True),
    )(column_map, codes, exponents)


def finish_kernel(count, order, *refs):
    arrived, (rollout, sums) = refs[:count], refs[count:]
    rows = arrived[0].shape[-1]
    blocks = rows // BLOCK
    row_block = lax.broadcasted_iota(jnp.int32, (rows, blocks * count), 0) // BLOCK
    column = lax.broadcasted_iota(jnp.int32, (rows, blocks * count), 1)
    total = None
    for part in range(count):
        values = arrived[part][0, 0]
        rollout[0, :, part * rows : (part + 1) * rows] = values
        chooser = jnp.where(column == row_block + part * blocks, 1.0, 0.0).astype(jnp.bfloat16)
        term = jnp.dot(values, chooser, preferred_element_type=jnp.float32)
        total = term if total is None else total + term
    sums[0] = total


def finish(arrived, row_order):
    devices, layers, col_width, rows = arrived.shape
    blocks = rows // BLOCK
    count = max(1, LANES // blocks)
    if rows % LANES or blocks * count != LANES or devices % count or col_width % 16:
        rollout = jnp.take(arrived, row_order, axis=0).transpose(1, 2, 0, 3)
        rollout = rollout.reshape(layers, col_width, devices * rows)
        sums = rollout.astype(jnp.float32).reshape(layers, col_width, devices * blocks, BLOCK).sum(axis=-1)
        return rollout, sums

    def pick(part):
        return lambda layer, group, order: (order[group * count + part], layer, 0, 0)

    return pl.pallas_call(
        functools.partial(finish_kernel, count),
        grid_spec=pltpu.PrefetchScalarGridSpec(
            num_scalar_prefetch=1,
            grid=(layers, devices // count),
            in_specs=[pl.BlockSpec((1, 1, col_width, rows), pick(part)) for part in range(count)],
            out_specs=[
                pl.BlockSpec((1, col_width, count * rows), lambda layer, group, order: (layer, 0, group)),
                pl.BlockSpec((1, col_width, LANES), lambda layer, group, order: (layer, 0, group)),
            ],
        ),
        out_shape=[
            jax.ShapeDtypeStruct((layers, col_width, devices * rows), jnp.bfloat16),
            jax.ShapeDtypeStruct((layers, col_width, devices * blocks), jnp.float32),
        ],
    )(row_order, *([arrived] * count))


def shards(codes, exponents, column_map, row_order):
    grp_size = lax.axis_size("grp")
    devices = lax.axis_size("chain") * grp_size
    arrived = exchange(codes, exponents, column_map, devices, grp_size)
    rollout, sums = finish(arrived, row_order)
    return (rollout, sums)


def solution(mesh):
    return jax.shard_map(
        shards,
        mesh=mesh,
        in_specs=(P(None, ("chain", "grp"), None), P(None, ("chain", "grp"), None), P(), P()),
        out_specs=(P(None, ("chain", "grp"), None), P(None, ("chain", "grp"), None)),
        check_vma=False,
    )
```

profile of v0, /device:TPU:9, one launch (start us, length us, event | category | flops | bytes accessed | tf_op | source)
XLA Modules:
  0.0 305.9 jit_solution(5531018290373345067)
XLA Ops:
  0.6 291.2 %shard_map.59.refs_0_.refs_1_.refs_2_.refs_3_.refs_4_.refs_5_.refs_6_.refs_7_ = bf16[32,2,192,512]{3,2,1,0:T(8,128)(2,1)} custom-call(s32[32]{0:T(128)} %column_map.1, bf16[2,512,6144]{2,1,0:T(8,128)(2,1)} %codes.1, s32[2,16,6144]{2,1,0:T(8,128)} %exponents.1), custom_call_target="tpu_custom_call" | custom-call | tf_op jit(solution)/shard_map/pallas_call | solution.py:167
  291.9 14.0 %shard_map.60 = (bf16[2,192,16384]{2,1,0:T(8,128)(2,1)}, f32[2,192,512]{2,1,0:T(8,128)}) custom-call(s32[32]{0:T(128)} %order.1, bf16[32,2,192,512]{3,2,1,0:T(8,128)(2,1)} %shard_map.59.refs_0_.refs_1_.refs_2_.refs_3_.refs_4_.refs_5_.refs_6_.refs_7_, bf16[32,2,192,512]{3,2,1,0:T(8,128)(2,1)} %shard_map.59.refs_0_.refs_1_.refs_2_.refs_3_.refs_4_.refs_5_.refs_6_.refs_7_, ...), custom_call_target="tpu_custom_call" | custom-call | tf_op jit(solution)/shard_map/pallas_call | solution.py:215
where the time goes:
time: 306 us
  Pallas kernels  305 us (100%)
    pallas_call x1, Pallas kernels, exchange(): pl.pallas_call(functools.partial(fused_kernel, devices, grp_size), out_sh...  291 us
    pallas_call x1, Pallas kernels, finish(): pl.pallas_call(functools.partial(finish_kernel, count), grid_spec=pltpu.P...  14 us

commit v1 on v0

--- a/solution.py
+++ b/solution.py
@@ -68,7 +68,7 @@
 
 def fused_kernel(
     devices, grp_size, column_map, codes, exponents, arrived,
-    codes_in, exponents_in, turned, sending, load_sems, send_sems, recv_sems, own_sem,
+    codes_in, exponents_in, turned, sending, load_sems, send_sems, recv_sems,
 ):
     pairs, layers, rows, pair = codes_in.shape
     col_width = pair // 2
@@ -119,9 +119,7 @@
 
     fill(0)
     traffic.send(turn_of(devices - 2, devices)).start()
-    own = pltpu.make_async_copy(sending.at[0], arrived.at[traffic.me], own_sem)
-    own.start()
-    own.wait()
+    arrived[traffic.me] = sending[0]
     traffic.finish()
 
 
@@ -166,9 +164,9 @@
     pairs = devices // 2
     return pl.pallas_call(
         functools.partial(fused_kernel, devices, grp_size),
-        out_shape=shape,
+        out_shape=pltpu.VMEM((devices, *block), jnp.bfloat16),
         in_specs=[pl.BlockSpec(memory_space=pltpu.SMEM), anywhere, anywhere],
-        out_specs=anywhere,
+        out_specs=pl.BlockSpec(memory_space=pltpu.VMEM),
         scratch_shapes=[
             pltpu.VMEM((pairs, layers, rows, 2 * col_width), codes.dtype),
             pltpu.VMEM((pairs, layers, rows // BLOCK, 2 * col_width), exponents.dtype),
@@ -177,26 +175,47 @@
             pltpu.SemaphoreType.DMA((2, pairs)),
             peers,
             peers,
-            pltpu.SemaphoreType.DMA,
         ],
-        compiler_params=pltpu.CompilerParams(has_side_effects=True),
+        compiler_params=pltpu.CompilerParams(has_side_effects=True, vmem_limit_bytes=44 << 20),
     )(column_map, codes, exponents)
 
 
-def finish_kernel(count, order, *refs):
-    arrived, (rollout, sums) = refs[:count], refs[count:]
-    rows = arrived[0].shape[-1]
+def deliver_kernel(order, arrived, rollout, sums, sums_out, block_sems, sums_sem):
+    devices, layers, col_width, rows = arrived.shape
     blocks = rows // BLOCK
-    row_block = lax.broadcasted_iota(jnp.int32, (rows, blocks * count), 0) // BLOCK
-    column = lax.broadcasted_iota(jnp.int32, (rows, blocks * count), 1)
-    total = None
-    for part in range(count):
-        values = arrived[part][0, 0]
-        rollout[0, :, part * rows : (part + 1) * rows] = values
-        chooser = jnp.where(column == row_block + part * blocks, 1.0, 0.0).astype(jnp.bfloat16)
-        term = jnp.dot(values, chooser, preferred_element_type=jnp.float32)
-        total = term if total is None else total + term
-    sums[0] = total
+    count = LANES // blocks
+
+    def place(slot):
+        columns = pl.ds(pl.multiple_of(slot * rows, LANES), rows)
+        return pltpu.make_async_copy(arrived.at[order[slot]], rollout.at[:, :, columns], block_sems.at[slot])
+
+    @pl.loop(0, devices)
+    def _(slot):
+        place(slot).start()
+
+    row_block = lax.broadcasted_iota(jnp.int32, (rows, LANES), 0) // BLOCK
+    column = lax.broadcasted_iota(jnp.int32, (rows, LANES), 1)
+    choosers = [
+        jnp.where(column == row_block + part * blocks, 1.0, 0.0).astype(jnp.bfloat16) for part in range(count)
+    ]
+
+    for group in range(devices // count):
+        for layer in range(layers):
+            total = None
+            for part in range(count):
+                values = arrived[order[group * count + part], layer]
+                term = jnp.dot(values, choosers[part], preferred_element_type=jnp.float32)
+                total = term if total is None else total + term
+            sums_out[layer, :, group * LANES : (group + 1) * LANES] = total
+
+    out = pltpu.make_async_copy(sums_out, sums, sums_sem)
+    out.start()
+
+    @pl.loop(0, devices)
+    def _(slot):
+        place(slot).wait()
+
+    out.wait()
 
 
 def finish(arrived, row_order):
@@ -208,26 +227,24 @@
         rollout = rollout.reshape(layers, col_width, devices * rows)
         sums = rollout.astype(jnp.float32).reshape(layers, col_width, devices * blocks, BLOCK).sum(axis=-1)
         return rollout, sums
-
-    def pick(part):
-        return lambda layer, group, order: (order[group * count + part], layer, 0, 0)
-
+    sums_shape = (layers, col_width, devices * blocks)
+    anywhere = pl.BlockSpec(memory_space=pl.ANY)
+    arrived = pltpu.with_memory_space_constraint(arrived, pltpu.VMEM)
     return pl.pallas_call(
-        functools.partial(finish_kernel, count),
-        grid_spec=pltpu.PrefetchScalarGridSpec(
-            num_scalar_prefetch=1,
-            grid=(layers, devices // count),
-            in_specs=[pl.BlockSpec((1, 1, col_width, rows), pick(part)) for part in range(count)],
-            out_specs=[
-                pl.BlockSpec((1, col_width, count * rows), lambda layer, group, order: (layer, 0, group)),
-                pl.BlockSpec((1, col_width, LANES), lambda layer, group, order: (layer, 0, group)),
-            ],
-        ),
+        deliver_kernel,
         out_shape=[
             jax.ShapeDtypeStruct((layers, col_width, devices * rows), jnp.bfloat16),
-            jax.ShapeDtypeStruct((layers, col_width, devices * blocks), jnp.float32),
+            jax.ShapeDtypeStruct(sums_shape, jnp.float32),
         ],
-    )(row_order, *([arrived] * count))
+        in_specs=[pl.BlockSpec(memory_space=pltpu.SMEM), pl.BlockSpec(memory_space=pltpu.VMEM)],
+        out_specs=[anywhere, anywhere],
+        scratch_shapes=[
+            pltpu.VMEM(sums_shape, jnp.float32),
+            pltpu.SemaphoreType.DMA((devices,)),
+            pltpu.SemaphoreType.DMA,
+        ],
+        compiler_params=pltpu.CompilerParams(vmem_limit_bytes=16 << 20),
+    )(row_order, arrived)
 
 
 def shards(codes, exponents, column_map, row_order):

time: 306 us -> 298 us (0.974)
  Pallas kernels: 305 us -> 297 us
    pallas_call x1, Pallas kernels: 14 us -> 5.61 us  [finish(): pl.pallas_call(deliver_kernel, out_shape=[jax.ShapeDtypeStruct((layers, c...]
where the time goes in v1:
time: 298 us; the launch traced here: 297 us
  Pallas kernels  297 us (100%)
    pallas_call x1, Pallas kernels, exchange(): pl.pallas_call(functools.partial(fused_kernel, devices, grp_size), out_sh...  291 us

profile of v1, /device:TPU:9, one launch (start us, length us, event | category | flops | bytes accessed | tf_op | source)
XLA Modules:
  0.0 297.4 jit_solution(15216055289339725992)
XLA Ops:
  0.6 0.0 copy-start
  0.6 291.1 %shard_map.59.arrived = bf16[32,2,192,512]{3,2,1,0:T(8,128)(2,1)S(1)} custom-call(s32[32]{0:T(128)} %column_map.1, bf16[2,512,6144]{2,1,0:T(8,128)(2,1)} %codes.1, s32[2,16,6144]{2,1,0:T(8,128)} %exponents.1), custom_call_target="tpu_custom_call" | custom-call | tf_op jit(solution)/shard_map/pallas_call | solution.py:165
  291.8 0.0 copy-done
  291.8 5.6 %shard_map.60 = (bf16[2,192,16384]{2,1,0:T(8,128)(2,1)}, f32[2,192,512]{2,1,0:T(8,128)}) custom-call(s32[32]{0:T(128)S(1)} %copy-done, bf16[32,2,192,512]{3,2,1,0:T(8,128)(2,1)S(1)} %shard_map.59.arrived), custom_call_target="tpu_custom_call" | custom-call | tf_op jit(solution)/shard_map/pallas_call | solution.py:233
Async XLA Ops:
  0.6 291.1 %copy-start = (s32[32]{0:T(128)S(1)}, s32[32]{0:T(128)}, u32[]{:S(2)}) copy-start(s32[32]{0:T(128)} %order.1) | copy-start | bytes 388

commit v2 on v1

v2 whole, which is shorter than its diff:
```python
import functools

import jax
import jax.numpy as jnp
from jax import lax
from jax.experimental import pallas as pl
from jax.experimental.pallas import tpu as pltpu
from jax.sharding import PartitionSpec as P

MESH = pl.DeviceIdType.MESH
BLOCK = 32
LANES = 128
EARLY = 2


def partner(me, step, devices):
    if devices & (devices - 1):
        return lax.rem(me + step, devices)
    peer, bit = 0, 1
    while bit < devices:
        peer = peer + lax.rem(me // bit + step // bit, 2) * bit
        bit *= 2
    return peer


def origin(me, step, devices):
    if devices & (devices - 1):
        return lax.rem(me - step + devices, devices)
    return partner(me, step, devices)


def turn_of(index, devices):
    half = devices // 2
    return jnp.where(index < devices - half, index + half, index - (devices - half) + 1)


class Traffic:
    def __init__(self, devices, grp_size, pieces, source, arrived, send_sems, recv_sems):
        self.devices, self.grp_size, self.pieces = devices, grp_size, pieces
        self.source, self.arrived = source, arrived
        self.send_sems, self.recv_sems = send_sems, recv_sems
        self.me = lax.axis_index("chain") * grp_size + lax.axis_index("grp")

    def place(self, other):
        return (other // self.grp_size, lax.rem(other, self.grp_size))

    def copy(self, step, piece, other, slot):
        return pltpu.make_async_remote_copy(
            src_ref=self.source(step, piece, other),
            dst_ref=self.arrived.at[slot] if self.pieces == 1 else self.arrived.at[slot, piece],
            send_sem=self.send_sems.at[step, piece],
            recv_sem=self.recv_sems.at[step, piece],
            device_id=self.place(other),
            device_id_type=MESH,
        )

    def send(self, step, piece):
        return self.copy(step, piece, partner(self.me, step, self.devices), self.me)

    def greet(self):
        barrier = pltpu.get_barrier_semaphore()

        @pl.loop(1, self.devices)
        def _(step):
            other = self.place(partner(self.me, step, self.devices))
            pl.semaphore_signal(barrier, inc=1, device_id=other, device_id_type=MESH)

    def greeted(self):
        pl.semaphore_wait(pltpu.get_barrier_semaphore(), self.devices - 1)

    def finish(self):
        @pl.loop(1, self.devices)
        def _(step):
            sender = origin(self.me, step, self.devices)
            for piece in range(self.pieces):
                self.copy(step, piece, sender, sender).wait_recv()

        @pl.loop(1, self.devices)
        def _(step):
            for piece in range(self.pieces):
                self.send(step, piece).wait_send()


def fused_kernel(devices, grp_size, layers, column_map_in, row_order_in, codes, exponents, arrived, row_order, column_map, map_sem, order_sem, *scratch):
    codes_in, exponents_in = scratch[:layers], scratch[layers : 2 * layers]
    turned, sending, load_sems, send_sems, recv_sems = scratch[2 * layers :]
    pairs, rows, pair = codes_in[0].shape
    col_width = pair // 2
    traffic = Traffic(
        devices, grp_size, layers, lambda step, piece, other: sending.at[step, piece], arrived, send_sems, recv_sems
    )

    def loads(layer, index):
        columns = pl.ds(pl.multiple_of(index * pair, LANES), pair)
        return (
            pltpu.make_async_copy(
                exponents.at[layer, :, columns], exponents_in[layer].at[index], load_sems.at[0, layer, index]
            ),
            pltpu.make_async_copy(codes.at[layer, :, columns], codes_in[layer].at[index], load_sems.at[1, layer, index]),
        )

    def start_loads(layer):
        @pl.loop(0, pairs)
        def _(index):
            for load in loads(layer, index):
                load.start()

    def wait_loads(layer):
        @pl.loop(0, pairs)
        def _(index):
            for load in loads(layer, index):
                load.wait()

    def fill(step, layer, out):
        column = column_map[partner(traffic.me, step, devices)]
        which = column // 2
        scaling = jnp.exp2(exponents_in[layer][which].astype(jnp.float32)).astype(jnp.bfloat16)
        for first in range(0, rows, LANES):
            pieces = []
            for row in range(first, first + LANES, BLOCK):
                block = row // BLOCK
                values = codes_in[layer][which, row : row + BLOCK, :]
                pieces.append(values * scaling[block : block + 1, :])
            both = jnp.concatenate(pieces, axis=0).T
            turned[0, :, first : first + LANES] = both[:col_width]
            turned[1, :, first : first + LANES] = both[col_width:]
        out[...] = turned[lax.rem(column, 2)]

    def prepare(index, layer):
        step = turn_of(index, devices)
        fill(step, layer, sending.at[step, layer])

    def send(index, layer):
        traffic.send(turn_of(index, devices), layer).start()

    def send_before(index, layer):
        if layer:
            send(index, layer - 1)
        else:
            send(index - 1, layers - 1)

    early = min(EARLY, devices - 1)
    mapping = pltpu.make_async_copy(column_map_in, column_map, map_sem)
    mapping.start()
    ordering = pltpu.make_async_copy(row_order_in, row_order, order_sem)
    ordering.start()
    start_loads(0)
    traffic.greet()
    mapping.wait()
    ordering.wait()
    wait_loads(0)
    for layer in range(1, layers):
        start_loads(layer)

    @pl.loop(0, early)
    def _(index):
        prepare(index, 0)

    traffic.greeted()

    @pl.loop(0, early - 1)
    def _(index):
        send(index, 0)

    for layer in range(1, layers):
        wait_loads(layer)

        @pl.loop(0, early)
        def _(index):
            prepare(index, layer)

    send(early - 1, 0)
    for layer in range(1, layers):

        @pl.loop(0, early - (1 if layer == layers - 1 else 0))
        def _(index):
            send(index, layer)

    @pl.loop(early, devices - 1)
    def _(index):
        for layer in range(layers):
            prepare(index, layer)
            send_before(index, layer)

    for layer in range(layers):
        fill(0, layer, arrived.at[traffic.me, layer])
        if layer == 0:
            send(devices - 2, layers - 1)
    traffic.finish()


def exchange_kernel(devices, grp_size, outgoing, arrived, own, send_sems, recv_sems, own_sems):
    traffic = Traffic(
        devices, grp_size, 1, lambda step, piece, other: outgoing.at[other], arrived, send_sems, recv_sems
    )
    traffic.greet()
    traffic.greeted()

    @pl.loop(0, devices - 1)
    def _(index):
        traffic.send(turn_of(index, devices), 0).start()

    take = pltpu.make_async_copy(outgoing.at[traffic.me], own, own_sems.at[0])
    take.start()
    take.wait()
    put = pltpu.make_async_copy(own, arrived.at[traffic.me], own_sems.at[1])
    put.start()
    put.wait()
    traffic.finish()


def exchange(codes, exponents, column_map, row_order, devices, grp_size):
    layers, rows, width = codes.shape
    col_width = width // devices
    block = (layers, col_width, rows)
    anywhere = pl.BlockSpec(memory_space=pl.ANY)
    if col_width % 64 or rows % LANES or devices % 2:
        scaling = jnp.exp2(exponents.astype(jnp.float32))
        values = (codes.astype(jnp.float32) * jnp.repeat(scaling, BLOCK, axis=1)).astype(jnp.bfloat16)
        values = values.reshape(layers, rows, devices, col_width)
        outgoing = jnp.take(values.transpose(2, 0, 3, 1), column_map, axis=0)
        peers = pltpu.SemaphoreType.DMA((devices, 1))
        return pl.pallas_call(
            functools.partial(exchange_kernel, devices, grp_size),
            out_shape=jax.ShapeDtypeStruct((devices, *block), jnp.bfloat16),
            in_specs=[anywhere],
            out_specs=anywhere,
            scratch_shapes=[pltpu.VMEM(block, jnp.bfloat16), peers, peers, pltpu.SemaphoreType.DMA((2,))],
            compiler_params=pltpu.CompilerParams(has_side_effects=True, collective_id=0),
        )(outgoing), row_order
    peers = pltpu.SemaphoreType.DMA((devices, layers))
    return pl.pallas_call(
        functools.partial(fused_kernel, devices, grp_size, layers),
        out_shape=[
            pltpu.VMEM((devices, *block), jnp.bfloat16),
            pltpu.SMEM(row_order.shape, row_order.dtype),
        ],
        in_specs=[anywhere] * 4,
        out_specs=[pl.BlockSpec(memory_space=pltpu.VMEM), pl.BlockSpec(memory_space=pltpu.SMEM)],
        scratch_shapes=[
            pltpu.SMEM(column_map.shape, column_map.dtype),
            pltpu.SemaphoreType.DMA,
            pltpu.SemaphoreType.DMA,
            *[pltpu.VMEM((devices // 2, rows, 2 * col_width), codes.dtype)] * layers,
            *[pltpu.VMEM((devices // 2, rows // BLOCK, 2 * col_width), exponents.dtype)] * layers,
            pltpu.VMEM((2, col_width, rows), jnp.bfloat16),
            pltpu.VMEM((devices, *block), jnp.bfloat16),
            pltpu.SemaphoreType.DMA((2, layers, devices // 2)),
            peers,
            peers,
        ],
        compiler_params=pltpu.CompilerParams(
            has_side_effects=True, collective_id=0, vmem_limit_bytes=44 << 20
        ),
    )(column_map, row_order, codes, exponents)


def deliver_kernel(order, arrived, rollout, sums, sums_out, block_sems, sums_sem):
    devices, layers, col_width, rows = arrived.shape
    blocks = rows // BLOCK
    count = LANES // blocks

    def place(slot):
        columns = pl.ds(pl.multiple_of(slot * rows, LANES), rows)
        return pltpu.make_async_copy(arrived.at[order[slot]], rollout.at[:, :, columns], block_sems.at[slot])

    @pl.loop(0, devices)
    def _(slot):
        place(slot).start()

    row_block = lax.broadcasted_iota(jnp.int32, (rows, LANES), 0) // BLOCK
    column = lax.broadcasted_iota(jnp.int32, (rows, LANES), 1)
    choosers = [
        jnp.where(column == row_block + part * blocks, 1.0, 0.0).astype(jnp.bfloat16) for part in range(count)
    ]

    for group in range(devices // count):
        for layer in range(layers):
            total = None
            for part in range(count):
                values = arrived[order[group * count + part], layer]
                term = jnp.dot(values, choosers[part], preferred_element_type=jnp.float32)
                total = term if total is None else total + term
            sums_out[layer, :, group * LANES : (group + 1) * LANES] = total

    out = pltpu.make_async_copy(sums_out, sums, sums_sem)
    out.start()

    @pl.loop(0, devices)
    def _(slot):
        place(slot).wait()

    out.wait()


def finish(arrived, row_order):
    devices, layers, col_width, rows = arrived.shape
    blocks = rows // BLOCK
    count = max(1, LANES // blocks)
    if rows % LANES or blocks * count != LANES or devices % count or col_width % 16:
        rollout = jnp.take(arrived, row_order, axis=0).transpose(1, 2, 0, 3)
        rollout = rollout.reshape(layers, col_width, devices * rows)
        sums = rollout.astype(jnp.float32).reshape(layers, col_width, devices * blocks, BLOCK).sum(axis=-1)
        return rollout, sums
    sums_shape = (layers, col_width, devices * blocks)
    anywhere = pl.BlockSpec(memory_space=pl.ANY)
    arrived = pltpu.with_memory_space_constraint(arrived, pltpu.VMEM)
    row_order = pltpu.with_memory_space_constraint(row_order, pltpu.SMEM)
    return pl.pallas_call(
        deliver_kernel,
        out_shape=[
            jax.ShapeDtypeStruct((layers, col_width, devices * rows), jnp.bfloat16),
            jax.ShapeDtypeStruct(sums_shape, jnp.float32),
        ],
        in_specs=[pl.BlockSpec(memory_space=pltpu.SMEM), pl.BlockSpec(memory_space=pltpu.VMEM)],
        out_specs=[anywhere, anywhere],
        scratch_shapes=[
            pltpu.VMEM(sums_shape, jnp.float32),
            pltpu.SemaphoreType.DMA((devices,)),
            pltpu.SemaphoreType.DMA,
        ],
        compiler_params=pltpu.CompilerParams(vmem_limit_bytes=16 << 20),
    )(row_order, arrived)


def shards(codes, exponents, column_map, row_order):
    grp_size = lax.axis_size("grp")
    devices = lax.axis_size("chain") * grp_size
    arrived, order = exchange(codes, exponents, column_map, row_order, devices, grp_size)
    rollout, sums = finish(arrived, order)
    return (rollout, sums)


def solution(mesh):
    return jax.shard_map(
        shards,
        mesh=mesh,
        in_specs=(P(None, ("chain", "grp"), None), P(None, ("chain", "grp"), None), P(), P()),
        out_specs=(P(None, ("chain", "grp"), None), P(None, ("chain", "grp"), None)),
        check_vma=False,
    )
```

time: 298 us -> 285 us (0.956)
  Pallas kernels: 297 us -> 284 us
    pallas_call x1, Pallas kernels: 291 us -> 279 us  [exchange(): pl.pallas_call(functools.partial(fused_kernel, devices, grp_size, layers)...]
where the time goes in v2:
time: 285 us
  Pallas kernels  284 us (100%)
    pallas_call x1, Pallas kernels, exchange(): pl.pallas_call(functools.partial(fused_kernel, devices, grp_size, layers)...  279 us

profile of v2, /device:TPU:9, one launch (start us, length us, event | category | flops | bytes accessed | tf_op | source)
XLA Modules:
  0.0 285.1 jit_solution(17531624386983968790)
XLA Ops:
  0.6 279.4 %shard_map.59 = (bf16[32,2,192,512]{3,2,1,0:T(8,128)(2,1)S(1)}, s32[32]{0:T(128)S(4)}) custom-call(s32[32]{0:T(128)} %column_map_in.1, s32[32]{0:T(128)} %row_order_in.1, bf16[2,512,6144]{2,1,0:T(8,128)(2,1)} %codes.1, s32[2,16,6144]{2,1,0:T(8,128)} %exponents.1), custom_call_target="tpu_custom_call" | custom-call | tf_op jit(solution)/shard_map/pallas_call | solution.py:232
  280.0 5.1 %shard_map.60 = (bf16[2,192,16384]{2,1,0:T(8,128)(2,1)}, f32[2,192,512]{2,1,0:T(8,128)}) custom-call(s32[32]{0:T(128)S(4)} %get-tuple-element.4.order, bf16[32,2,192,512]{3,2,1,0:T(8,128)(2,1)S(1)} %get-tuple-element.5.arrived), custom_call_target="tpu_custom_call" | custom-call | tf_op jit(solution)/shard_map/pallas_call | solution.py:309

commit v3 on v2

--- a/solution.py
+++ b/solution.py
@@ -10,23 +10,6 @@
 MESH = pl.DeviceIdType.MESH
 BLOCK = 32
 LANES = 128
-EARLY = 2
-
-
-def partner(me, step, devices):
-    if devices & (devices - 1):
-        return lax.rem(me + step, devices)
-    peer, bit = 0, 1
-    while bit < devices:
-        peer = peer + lax.rem(me // bit + step // bit, 2) * bit
-        bit *= 2
-    return peer
-
-
-def origin(me, step, devices):
-    if devices & (devices - 1):
-        return lax.rem(me - step + devices, devices)
-    return partner(me, step, devices)
 
 
 def turn_of(index, devices):
@@ -40,6 +23,21 @@
         self.source, self.arrived = source, arrived
         self.send_sems, self.recv_sems = send_sems, recv_sems
         self.me = lax.axis_index("chain") * grp_size + lax.axis_index("grp")
+        self.flips = []
+        bit = 1
+        while bit < devices and not devices & (devices - 1):
+            self.flips.append((bit, bit - 2 * bit * lax.rem(self.me // bit, 2)))
+            bit *= 2
+
+    def partner(self, step):
+        if not self.flips:
+            return lax.rem(self.me + step, self.devices)
+        if isinstance(step, int):
+            return self.me + sum(flip for bit, flip in self.flips if step & bit)
+        return self.me + sum(lax.rem(step // bit, 2) * flip for bit, flip in self.flips)
+
+    def origin(self, step):
+        return self.partner(step) if self.flips else lax.rem(self.me - step + self.devices, self.devices)
 
     def place(self, other):
         return (other // self.grp_size, lax.rem(other, self.grp_size))
@@ -55,14 +53,13 @@
         )
 
     def send(self, step, piece):
-        return self.copy(step, piece, partner(self.me, step, self.devices), self.me)
+        return self.copy(step, piece, self.partner(step), self.me)
 
     def greet(self):
         barrier = pltpu.get_barrier_semaphore()
 
-        @pl.loop(1, self.devices)
-        def _(step):
-            other = self.place(partner(self.me, step, self.devices))
+        for step in range(1, self.devices):
+            other = self.place(self.partner(step))
             pl.semaphore_signal(barrier, inc=1, device_id=other, device_id_type=MESH)
 
     def greeted(self):
@@ -71,50 +68,43 @@
     def finish(self):
         @pl.loop(1, self.devices)
         def _(step):
-            sender = origin(self.me, step, self.devices)
-            for piece in range(self.pieces):
-                self.copy(step, piece, sender, sender).wait_recv()
-
-        @pl.loop(1, self.devices)
-        def _(step):
+            sender = self.origin(step)
             for piece in range(self.pieces):
                 self.send(step, piece).wait_send()
-
-
-def fused_kernel(devices, grp_size, layers, column_map_in, row_order_in, codes, exponents, arrived, row_order, column_map, map_sem, order_sem, *scratch):
-    codes_in, exponents_in = scratch[:layers], scratch[layers : 2 * layers]
-    turned, sending, load_sems, send_sems, recv_sems = scratch[2 * layers :]
+                self.copy(step, piece, sender, sender).wait_recv()
+
+
+def fused_kernel(
+    devices, grp_size, layers, column_map_in, row_order_in, codes, exponents, arrived, row_order, column_map, *scratch
+):
+    codes_in, exponents_in, scalings = (scratch[group * layers : (group + 1) * layers] for group in range(3))
+    turned, sending, map_sems, load_sems, send_sems, recv_sems = scratch[3 * layers :]
     pairs, rows, pair = codes_in[0].shape
     col_width = pair // 2
     traffic = Traffic(
         devices, grp_size, layers, lambda step, piece, other: sending.at[step, piece], arrived, send_sems, recv_sems
     )
 
-    def loads(layer, index):
-        columns = pl.ds(pl.multiple_of(index * pair, LANES), pair)
-        return (
-            pltpu.make_async_copy(
-                exponents.at[layer, :, columns], exponents_in[layer].at[index], load_sems.at[0, layer, index]
-            ),
-            pltpu.make_async_copy(codes.at[layer, :, columns], codes_in[layer].at[index], load_sems.at[1, layer, index]),
-        )
-
-    def start_loads(layer):
-        @pl.loop(0, pairs)
-        def _(index):
-            for load in loads(layer, index):
-                load.start()
-
-    def wait_loads(layer):
-        @pl.loop(0, pairs)
-        def _(index):
-            for load in loads(layer, index):
-                load.wait()
+    def columns_of(index):
+        return pl.ds(index * pair, pair)
+
+    def loads(layer):
+        yield pltpu.make_async_copy(exponents.at[layer], exponents_in[layer], load_sems.at[layer, pairs])
+        for index in range(pairs):
+            source = codes.at[layer, :, columns_of(index)]
+            yield pltpu.make_async_copy(source, codes_in[layer].at[index], load_sems.at[layer, index])
+
+    def loaded(layer):
+        for load in loads(layer):
+            load.wait()
+        for index in range(pairs):
+            powers = jnp.exp2(exponents_in[layer][:, columns_of(index)].astype(jnp.float32))
+            scalings[layer][index] = powers.astype(jnp.bfloat16)
 
     def fill(step, layer, out):
-        column = column_map[partner(traffic.me, step, devices)]
+        column = column_map[traffic.partner(step)]
         which = column // 2
-        scaling = jnp.exp2(exponents_in[layer][which].astype(jnp.float32)).astype(jnp.bfloat16)
+        scaling = scalings[layer][which]
         for first in range(0, rows, LANES):
             pieces = []
             for row in range(first, first + LANES, BLOCK):
@@ -133,54 +123,37 @@
     def send(index, layer):
         traffic.send(turn_of(index, devices), layer).start()
 
-    def send_before(index, layer):
-        if layer:
-            send(index, layer - 1)
-        else:
-            send(index - 1, layers - 1)
-
-    early = min(EARLY, devices - 1)
-    mapping = pltpu.make_async_copy(column_map_in, column_map, map_sem)
+    mapping = pltpu.make_async_copy(column_map_in, column_map, map_sems.at[0])
+    ordering = pltpu.make_async_copy(row_order_in, row_order, map_sems.at[1])
     mapping.start()
-    ordering = pltpu.make_async_copy(row_order_in, row_order, order_sem)
+    traffic.greet()
+    for load in loads(0):
+        load.start()
     ordering.start()
-    start_loads(0)
-    traffic.greet()
     mapping.wait()
+    loaded(0)
+    for layer in range(1, layers):
+        for load in loads(layer):
+            load.start()
+    prepare(0, 0)
+    prepare(1, 0)
+    traffic.greeted()
+    send(0, 0)
+    for layer in range(1, layers):
+        loaded(layer)
+        for index in range(2):
+            prepare(index, layer)
+            send(1 - index, layer - 1 + index)
     ordering.wait()
-    wait_loads(0)
-    for layer in range(1, layers):
-        start_loads(layer)
-
-    @pl.loop(0, early)
-    def _(index):
-        prepare(index, 0)
-
-    traffic.greeted()
-
-    @pl.loop(0, early - 1)
-    def _(index):
-        send(index, 0)
-
-    for layer in range(1, layers):
-        wait_loads(layer)
-
-        @pl.loop(0, early)
-        def _(index):
-            prepare(index, layer)
-
-    send(early - 1, 0)
-    for layer in range(1, layers):
-
-        @pl.loop(0, early - (1 if layer == layers - 1 else 0))
-        def _(index):
-            send(index, layer)
-
-    @pl.loop(early, devices - 1)
+
+    @pl.loop(2, devices - 1)
     def _(index):
         for layer in range(layers):
             prepare(index, layer)
-            send_before(index, layer)
+            if layer:
+                send(index, layer - 1)
+            else:
+                send(index - 1, layers - 1)
 
     for layer in range(layers):
         fill(0, layer, arrived.at[traffic.me, layer])
@@ -239,13 +212,13 @@
         out_specs=[pl.BlockSpec(memory_space=pltpu.VMEM), pl.BlockSpec(memory_space=pltpu.SMEM)],
         scratch_shapes=[
             pltpu.SMEM(column_map.shape, column_map.dtype),
-            pltpu.SemaphoreType.DMA,
-            pltpu.SemaphoreType.DMA,
             *[pltpu.VMEM((devices // 2, rows, 2 * col_width), codes.dtype)] * layers,
-            *[pltpu.VMEM((devices // 2, rows // BLOCK, 2 * col_width), exponents.dtype)] * layers,
+            *[pltpu.VMEM((rows // BLOCK, width), exponents.dtype)] * layers,
+            *[pltpu.VMEM((devices // 2, rows // BLOCK, 2 * col_width), jnp.bfloat16)] * layers,
             pltpu.VMEM((2, col_width, rows), jnp.bfloat16),
             pltpu.VMEM((devices, *block), jnp.bfloat16),
-            pltpu.SemaphoreType.DMA((2, layers, devices // 2)),
+            pltpu.SemaphoreType.DMA((2,)),
+            pltpu.SemaphoreType.DMA((layers, devices // 2 + 1)),
             peers,
             peers,
         ],

time: 285 us -> 285 us (level)
  no operation moved by 1% of the time
where the time goes in v3:
time: 285 us
  Pallas kernels  284 us (100%)
    pallas_call x1, Pallas kernels, exchange(): pl.pallas_call(functools.partial(fused_kernel, devices, grp_size, layers)...  279 us

profile of v3, /device:TPU:9, one launch (start us, length us, event | category | flops | bytes accessed | tf_op | source)
XLA Modules:
  0.0 284.7 jit_solution(7601720997957541559)
XLA Ops:
  0.6 279.0 %shard_map.59 = (bf16[32,2,192,512]{3,2,1,0:T(8,128)(2,1)S(1)}, s32[32]{0:T(128)S(4)}) custom-call(s32[32]{0:T(128)} %column_map_in.1, s32[32]{0:T(128)} %row_order_in.1, bf16[2,512,6144]{2,1,0:T(8,128)(2,1)} %codes.1, s32[2,16,6144]{2,1,0:T(8,128)} %exponents.1), custom_call_target="tpu_custom_call" | custom-call | tf_op jit(solution)/shard_map/pallas_call | solution.py:205
  279.6 5.1 %shard_map.60 = (bf16[2,192,16384]{2,1,0:T(8,128)(2,1)}, f32[2,192,512]{2,1,0:T(8,128)}) custom-call(s32[32]{0:T(128)S(4)} %get-tuple-element.4.order, bf16[32,2,192,512]{3,2,1,0:T(8,128)(2,1)S(1)} %get-tuple-element.5.arrived), custom_call_target="tpu_custom_call" | custom-call | tf_op jit(solution)/shard_map/pallas_call | solution.py:282

commit v4 on v3

--- a/solution.py
+++ b/solution.py
@@ -18,10 +18,10 @@
 
 
 class Traffic:
-    def __init__(self, devices, grp_size, pieces, source, arrived, send_sems, recv_sems):
+    def __init__(self, devices, grp_size, pieces, source, arrived, send_sem, recv_sem):
         self.devices, self.grp_size, self.pieces = devices, grp_size, pieces
         self.source, self.arrived = source, arrived
-        self.send_sems, self.recv_sems = send_sems, recv_sems
+        self.send_sem, self.recv_sem = send_sem, recv_sem
         self.me = lax.axis_index("chain") * grp_size + lax.axis_index("grp")
         self.flips = []
         bit = 1
@@ -46,8 +46,8 @@
         return pltpu.make_async_remote_copy(
             src_ref=self.source(step, piece, other),
             dst_ref=self.arrived.at[slot] if self.pieces == 1 else self.arrived.at[slot, piece],
-            send_sem=self.send_sems.at[step, piece],
-            recv_sem=self.recv_sems.at[step, piece],
+            send_sem=self.send_sem,
+            recv_sem=self.recv_sem,
             device_id=self.place(other),
             device_id_type=MESH,
         )
@@ -65,41 +65,46 @@
     def greeted(self):
         pl.semaphore_wait(pltpu.get_barrier_semaphore(), self.devices - 1)
 
-    def finish(self):
-        @pl.loop(1, self.devices)
-        def _(step):
-            sender = self.origin(step)
-            for piece in range(self.pieces):
-                self.send(step, piece).wait_send()
-                self.copy(step, piece, sender, sender).wait_recv()
+    def finish(self, blocks):
+        every = pl.ds(0, self.devices - 1)
+        total = pltpu.make_async_remote_copy(
+            src_ref=blocks.at[every],
+            dst_ref=self.arrived.at[every],
+            send_sem=self.send_sem,
+            recv_sem=self.recv_sem,
+            device_id=self.place(self.partner(1)),
+            device_id_type=MESH,
+        )
+        total.wait_send()
+        total.wait_recv()
 
 
 def fused_kernel(
     devices, grp_size, layers, column_map_in, row_order_in, codes, exponents, arrived, row_order, column_map, *scratch
 ):
     codes_in, exponents_in, scalings = (scratch[group * layers : (group + 1) * layers] for group in range(3))
-    turned, sending, map_sems, load_sems, send_sems, recv_sems = scratch[3 * layers :]
+    turned, sending, map_sems, load_sems, send_sem, recv_sem = scratch[3 * layers :]
     pairs, rows, pair = codes_in[0].shape
     col_width = pair // 2
     traffic = Traffic(
-        devices, grp_size, layers, lambda step, piece, other: sending.at[step, piece], arrived, send_sems, recv_sems
+        devices, grp_size, layers, lambda step, piece, other: sending.at[step, piece], arrived, send_sem, recv_sem
     )
 
     def columns_of(index):
         return pl.ds(index * pair, pair)
 
-    def loads(layer):
-        yield pltpu.make_async_copy(exponents.at[layer], exponents_in[layer], load_sems.at[layer, pairs])
+    def start_loads(layer):
+        pltpu.make_async_copy(exponents.at[layer], exponents_in[layer], load_sems.at[layer, 0]).start()
         for index in range(pairs):
             source = codes.at[layer, :, columns_of(index)]
-            yield pltpu.make_async_copy(source, codes_in[layer].at[index], load_sems.at[layer, index])
+            pltpu.make_async_copy(source, codes_in[layer].at[index], load_sems.at[layer, 1]).start()
 
     def loaded(layer):
-        for load in loads(layer):
-            load.wait()
+        pltpu.make_async_copy(exponents.at[layer], exponents_in[layer], load_sems.at[layer, 0]).wait()
         for index in range(pairs):
             powers = jnp.exp2(exponents_in[layer][:, columns_of(index)].astype(jnp.float32))
             scalings[layer][index] = powers.astype(jnp.bfloat16)
+        pltpu.make_async_copy(codes_in[layer], codes_in[layer], load_sems.at[layer, 1]).wait()
 
     def fill(step, layer, out):
         column = column_map[traffic.partner(step)]
@@ -127,14 +132,12 @@
     ordering = pltpu.make_async_copy(row_order_in, row_order, map_sems.at[1])
     mapping.start()
     traffic.greet()
-    for load in loads(0):
-        load.start()
+    start_loads(0)
     ordering.start()
     mapping.wait()
     loaded(0)
     for layer in range(1, layers):
-        for load in loads(layer):
-            load.start()
+        start_loads(layer)
     prepare(0, 0)
     prepare(1, 0)
     traffic.greeted()
@@ -159,12 +162,12 @@
         fill(0, layer, arrived.at[traffic.me, layer])
         if layer == 0:
             send(devices - 2, layers - 1)
-    traffic.finish()
-
-
-def exchange_kernel(devices, grp_size, outgoing, arrived, own, send_sems, recv_sems, own_sems):
+    traffic.finish(sending)
+
+
+def exchange_kernel(devices, grp_size, outgoing, arrived, own, send_sem, recv_sem, own_sems):
     traffic = Traffic(
-        devices, grp_size, 1, lambda step, piece, other: outgoing.at[other], arrived, send_sems, recv_sems
+        devices, grp_size, 1, lambda step, piece, other: outgoing.at[other], arrived, send_sem, recv_sem
     )
     traffic.greet()
     traffic.greeted()
@@ -179,7 +182,7 @@
     put = pltpu.make_async_copy(own, arrived.at[traffic.me], own_sems.at[1])
     put.start()
     put.wait()
-    traffic.finish()
+    traffic.finish(outgoing)
 
 
 def exchange(codes, exponents, column_map, row_order, devices, grp_size):
@@ -192,16 +195,18 @@
         values = (codes.astype(jnp.float32) * jnp.repeat(scaling, BLOCK, axis=1)).astype(jnp.bfloat16)
         values = values.reshape(layers, rows, devices, col_width)
         outgoing = jnp.take(values.transpose(2, 0, 3, 1), column_map, axis=0)
-        peers = pltpu.SemaphoreType.DMA((devices, 1))
         return pl.pallas_call(
             functools.partial(exchange_kernel, devices, grp_size),
             out_shape=jax.ShapeDtypeStruct((devices, *block), jnp.bfloat16),
             in_specs=[anywhere],
             out_specs=anywhere,
-            scratch_shapes=[pltpu.VMEM(block, jnp.bfloat16), peers, peers, pltpu.SemaphoreType.DMA((2,))],
+            scratch_shapes=[
+                pltpu.VMEM(block, jnp.bfloat16),
+                *[pltpu.SemaphoreType.DMA] * 2,
+                pltpu.SemaphoreType.DMA((2,)),
+            ],
             compiler_params=pltpu.CompilerParams(has_side_effects=True, collective_id=0),
         )(outgoing), row_order
-    peers = pltpu.SemaphoreType.DMA((devices, layers))
     return pl.pallas_call(
         functools.partial(fused_kernel, devices, grp_size, layers),
         out_shape=[
@@ -218,9 +223,8 @@
             pltpu.VMEM((2, col_width, rows), jnp.bfloat16),
             pltpu.VMEM((devices, *block), jnp.bfloat16),
             pltpu.SemaphoreType.DMA((2,)),
-            pltpu.SemaphoreType.DMA((layers, devices // 2 + 1)),
-            peers,
-            peers,
+            pltpu.SemaphoreType.DMA((layers, 2)),
+            *[pltpu.SemaphoreType.DMA] * 2,
         ],
         compiler_params=pltpu.CompilerParams(
             has_side_effects=True, collective_id=0, vmem_limit_bytes=44 << 20
@@ -228,14 +232,14 @@
     )(column_map, row_order, codes, exponents)
 
 
-def deliver_kernel(order, arrived, rollout, sums, sums_out, block_sems, sums_sem):
+def deliver_kernel(order, arrived, rollout, sums, sums_out, blocks_sem, sums_sem):
     devices, layers, col_width, rows = arrived.shape
     blocks = rows // BLOCK
     count = LANES // blocks
 
     def place(slot):
         columns = pl.ds(pl.multiple_of(slot * rows, LANES), rows)
-        return pltpu.make_async_copy(arrived.at[order[slot]], rollout.at[:, :, columns], block_sems.at[slot])
+        return pltpu.make_async_copy(arrived.at[order[slot]], rollout.at[:, :, columns], blocks_sem)
 
     @pl.loop(0, devices)
     def _(slot):
@@ -259,10 +263,7 @@
     out = pltpu.make_async_copy(sums_out, sums, sums_sem)
     out.start()
 
-    @pl.loop(0, devices)
-    def _(slot):
-        place(slot).wait()
-
+    pltpu.make_async_copy(rollout, rollout, blocks_sem).wait()
     out.wait()
 
 
@@ -289,7 +290,7 @@
         out_specs=[anywhere, anywhere],
         scratch_shapes=[
             pltpu.VMEM(sums_shape, jnp.float32),
-            pltpu.SemaphoreType.DMA((devices,)),
+            pltpu.SemaphoreType.DMA,
             pltpu.SemaphoreType.DMA,
         ],
         compiler_params=pltpu.CompilerParams(vmem_limit_bytes=16 << 20),

time: 285 us -> 283 us (level)
  no operation moved by 1% of the time
where the time goes in v4:
time: 283 us
  Pallas kernels  282 us (100%)
    pallas_call x1, Pallas kernels, exchange(): pl.pallas_call(functools.partial(fused_kernel, devices, grp_size, layers)...  278 us

profile of v4, /device:TPU:9, one launch (start us, length us, event | category | flops | bytes accessed | tf_op | source)
XLA Modules:
  0.0 283.0 jit_solution(17897152975614387442)
XLA Ops:
  0.6 277.5 %shard_map.59 = (bf16[32,2,192,512]{3,2,1,0:T(8,128)(2,1)S(1)}, s32[32]{0:T(128)S(4)}) custom-call(s32[32]{0:T(128)} %column_map_in.1, s32[32]{0:T(128)} %row_order_in.1, bf16[2,512,6144]{2,1,0:T(8,128)(2,1)} %codes.1, s32[2,16,6144]{2,1,0:T(8,128)} %exponents.1), custom_call_target="tpu_custom_call" | custom-call | tf_op jit(solution)/shard_map/pallas_call | solution.py:210
  278.2 4.8 %shard_map.60 = (bf16[2,192,16384]{2,1,0:T(8,128)(2,1)}, f32[2,192,512]{2,1,0:T(8,128)}) custom-call(s32[32]{0:T(128)S(4)} %get-tuple-element.4.order, bf16[32,2,192,512]{3,2,1,0:T(8,128)(2,1)S(1)} %get-tuple-element.5.arrived), custom_call_target="tpu_custom_call" | custom-call | tf_op jit(solution)/shard_map/pallas_call | solution.py:283

commit v5 on v4

--- a/solution.py
+++ b/solution.py
@@ -136,12 +136,12 @@
     ordering.start()
     mapping.wait()
     loaded(0)
-    for layer in range(1, layers):
-        start_loads(layer)
     prepare(0, 0)
     prepare(1, 0)
     traffic.greeted()
     send(0, 0)
+    for layer in range(1, layers):
+        start_loads(layer)
     for layer in range(1, layers):
         loaded(layer)
         for index in range(2):

time: 283 us -> 283 us (level)
  no operation moved by 1% of the time
where the time goes in v5:
time: 283 us
  Pallas kernels  282 us (100%)
    pallas_call x1, Pallas kernels, exchange(): pl.pallas_call(functools.partial(fused_kernel, devices, grp_size, layers)...  278 us

profile of v5, /device:TPU:9, one launch (start us, length us, event | category | flops | bytes accessed | tf_op | source)
XLA Modules:
  0.0 283.0 jit_solution(12431916890839949281)
XLA Ops:
  0.6 277.5 %shard_map.59 = (bf16[32,2,192,512]{3,2,1,0:T(8,128)(2,1)S(1)}, s32[32]{0:T(128)S(4)}) custom-call(s32[32]{0:T(128)} %column_map_in.1, s32[32]{0:T(128)} %row_order_in.1, bf16[2,512,6144]{2,1,0:T(8,128)(2,1)} %codes.1, s32[2,16,6144]{2,1,0:T(8,128)} %exponents.1), custom_call_target="tpu_custom_call" | custom-call | tf_op jit(solution)/shard_map/pallas_call | solution.py:210
  278.2 4.8 %shard_map.60 = (bf16[2,192,16384]{2,1,0:T(8,128)(2,1)}, f32[2,192,512]{2,1,0:T(8,128)}) custom-call(s32[32]{0:T(128)S(4)} %get-tuple-element.4.order, bf16[32,2,192,512]{3,2,1,0:T(8,128)(2,1)S(1)} %get-tuple-element.5.arrived), custom_call_target="tpu_custom_call" | custom-call | tf_op jit(solution)/shard_map/pallas_call | solution.py:283
